TPU v7x, 32 devices: a 4x4x1 block of a 4x4x8 slice. The times are simulated.
32 devices in a mesh: dp: 1 (over z), m3: 4 (over y), m2: 4 (over x), m1: 2 (over core).
Axes of the slice: x: 4, y: 4, z: 1, core: 2. Of those that a mesh axis runs over, the one named last changes fastest.
The devices are a block of a 4x4x8 slice.
Arguments:
- volume: bfloat16 [256, 64, 64, 64], P('dp', 'm1', 'm2', 'm3')
- fac_one: bfloat16 [64, 64], replicated
- fac_two: bfloat16 [64, 64], replicated
- fac_three: bfloat16 [64, 64], replicated
- diag_scale: float32 [64, 64, 64], P('m2', 'm1')
Outputs:
- output: bfloat16 [256, 64, 64, 64], P(('dp', 'm3'), 'm2', 'm1')
All inputs are finite; a program needn't handle non-finite values.
Results may differ from a plain program's by a relative error of at most 0.00844122.
Values are sent between devices in bfloat16 or wider.
A program may use at most 768 MiB of HBM per device.

v0:
```python
import jax
import jax.numpy as jnp
from jax import lax
from jax.sharding import PartitionSpec as P


def solution(mesh):
    def local_step(vol_blk, fac_one, fac_two, fac_three, diag_blk):
        full_three = lax.all_to_all(vol_blk, "m3", 0, 3, tiled=True)
        prod_three = lax.dot_general(full_three, fac_three, (((3,), (1,)), ((), ())), preferred_element_type=jnp.float32).astype(jnp.bfloat16)
        full_two = lax.all_to_all(prod_three, "m2", 3, 2, tiled=True)
        prod_two = lax.dot_general(full_two, fac_two, (((2,), (1,)), ((), ())), preferred_element_type=jnp.float32).astype(jnp.bfloat16)
        full_one = lax.all_to_all(prod_two, "m1", 3, 1, tiled=True)
        prod_one = lax.dot_general(full_one, fac_one, (((1,), (1,)), ((), ())), preferred_element_type=jnp.float32).astype(jnp.bfloat16)
        return (diag_blk[None] * prod_one.astype(jnp.float32)).astype(jnp.bfloat16)

    return jax.shard_map(local_step, mesh=mesh, in_specs=(P("dp", "m1", "m2", "m3"), P(), P(), P(), P("m2", "m1", None)), out_specs=P(("dp", "m3"), "m2", "m1", None), check_vma=False)
```

profile of v0, /device:TPU:97, one launch (start us, length us, event | category | flops | bytes accessed | tf_op | source)
XLA Modules:
  0.0 364.3 jit_solution(7001521840912542652)
XLA Ops:
  0.0 28.6 %copy.40 = bf16[256,32,16,16]{1,3,2,0:T(8,128)(2,1)} copy(bf16[256,32,16,16]{0,3,2,1:T(8,128)(2,1)} %param.5) | data formatting | bytes 8388608 | tf_op args[0]
  28.6 19.2 %reshape.4 = bf16[4,2,262144]{2,1,0:T(2,128)(2,1)} reshape(bf16[256,16,16,32]{3,2,1,0:T(8,128)(2,1)} %bitcast.35) | data formatting | bytes 8388608
  47.8 56.4 %all_to_all.54 = bf16[4,2,262144]{2,1,0:T(2,128)(2,1)} all-to-all(bf16[4,2,262144]{2,1,0:T(2,128)(2,1)} %reshape.4), channel_id=1, replica_groups=mesh['dp'=1,'m3'=4,'m2'=4,'m1'=2] {'m3'}, dimensions={0} | all-to-all | bytes 8388608 | tf_op jit(solution)/shard_map/all_to_all | solution.py:9
  104.2 12.0 %reshape.5 = bf16[256,16,16,32]{3,2,1,0:T(8,128)(2,1)} reshape(bf16[4,2,262144]{2,1,0:T(2,128)(2,1)} %all_to_all.54) | data formatting | bytes 8388608
  116.2 29.0 %copy.57 = bf16[4,64,32,16,16]{1,0,4,3,2:T(4,128)(2,1)} copy(bf16[4,64,32,16,16]{2,4,3,1,0:T(8,128)(2,1)} %bitcast.34) | data formatting | bytes 8388608 | tf_op jit(solution)/shard_map/all_to_all | solution.py:9
  145.3 9.3 %copy.42 = bf16[64,32,16,4,16]{0,4,3,2,1:T(8,128)(2,1)} copy(bf16[64,32,16,4,16]{0,3,4,2,1:T(4,128)(2,1)} %bitcast.36) | data formatting | bytes 8388608 | tf_op jit(solution)/shard_map/all_to_all | solution.py:9
  154.6 9.2 %convolution_convert_fusion = bf16[64,32,16,64]{3,0,2,1:T(8,128)(2,1)} fusion(bf16[64,32,16,64]{0,3,2,1:T(8,128)(2,1)} %bitcast.33, bf16[64,64]{1,0:T(8,128)(2,1)S(1)} %copy-done), kind=kOutput, calls=%fused_computation.6 | convolution fusion | flops 270532608 | bytes 8396800 | tf_op jit(solution)/shard_map/dot_general | solution.py:10
  163.8 12.5 %copy.44 = bf16[64,32,16,64]{0,2,1,3:T(8,128)(2,1)} copy(bf16[64,32,16,64]{3,0,2,1:T(8,128)(2,1)} %convolution_convert_fusion) | data formatting | bytes 8388608 | tf_op jit(solution)/shard_map/convert_element_type | solution.py:10
  176.3 9.5 %reshape.6 = bf16[4,2,262144]{2,1,0:T(2,128)(2,1)} reshape(bf16[64,32,16,64]{3,2,1,0:T(8,128)(2,1)} %bitcast.39) | data formatting | bytes 8388608
  185.8 53.4 %all_to_all.55 = bf16[4,2,262144]{2,1,0:T(2,128)(2,1)} all-to-all(bf16[4,2,262144]{2,1,0:T(2,128)(2,1)} %reshape.6), channel_id=1, replica_groups=mesh['dp'=1,'m3'=4,'m2'=4,'m1'=2] {'m2'}, dimensions={0} | all-to-all | bytes 8388608 | tf_op jit(solution)/shard_map/all_to_all | solution.py:11
  239.2 9.5 %reshape.7 = bf16[64,32,16,64]{3,2,1,0:T(8,128)(2,1)} reshape(bf16[4,2,262144]{2,1,0:T(2,128)(2,1)} %all_to_all.55) | data formatting | bytes 8388608
  248.7 0.0 copy-start.3
  248.7 16.3 %copy.46 = bf16[64,32,4,16,16]{0,4,3,2,1:T(8,128)(2,1)} copy(bf16[64,32,4,16,16]{0,3,1,4,2:T(8,128)(2,1)} %bitcast.40) | data formatting | bytes 8388608 | tf_op jit(solution)/shard_map/all_to_all | solution.py:11
  265.0 0.0 copy-done.3
  265.0 9.6 %fusion.4 = bf16[64,32,16,64]{3,0,2,1:T(8,128)(2,1)} fusion(bf16[64,32,64,16]{0,3,2,1:T(8,128)(2,1)} %bitcast.37, bf16[64,64]{1,0:T(8,128)(2,1)S(1)} %copy-done.3), kind=kOutput, calls=%fused_computation.5 | convolution fusion | flops 270532608 | bytes 8396800 | tf_op jit(solution)/shard_map/dot_general | solution.py:12
  274.6 12.5 %copy.48 = bf16[64,32,16,64]{0,2,1,3:T(8,128)(2,1)} copy(bf16[64,32,16,64]{3,0,2,1:T(8,128)(2,1)} %fusion.4) | data formatting | bytes 8388608 | tf_op jit(solution)/shard_map/convert_element_type | solution.py:12
  287.1 10.0 %reshape.8 = bf16[2,2,524288]{2,1,0:T(2,128)(2,1)} reshape(bf16[64,32,16,64]{3,2,1,0:T(8,128)(2,1)} %bitcast.41) | data formatting | bytes 8388608
  297.1 13.2 %all_to_all.56 = bf16[2,2,524288]{2,1,0:T(2,128)(2,1)} all-to-all(bf16[2,2,524288]{2,1,0:T(2,128)(2,1)} %reshape.8), channel_id=1, replica_groups=mesh['dp'=1,'m3'=4,'m2'=4,'m1'=2] {'m1'}, dimensions={0} | all-to-all | bytes 8388608 | tf_op jit(solution)/shard_map/all_to_all | solution.py:13
  310.3 10.0 %reshape.9 = bf16[64,32,16,64]{3,2,1,0:T(8,128)(2,1)} reshape(bf16[2,2,524288]{2,1,0:T(2,128)(2,1)} %all_to_all.56) | data formatting | bytes 8388608
  320.3 0.0 copy-start.2
  320.3 0.0 copy-start.4
  320.3 16.3 %copy.50 = bf16[64,2,32,16,32]{0,4,3,2,1:T(8,128)(2,1)} copy(bf16[64,2,32,16,32]{0,3,2,4,1:T(8,128)(2,1)} %bitcast.42) | data formatting | bytes 8388608 | tf_op jit(solution)/shard_map/all_to_all | solution.py:13
  336.6 15.3 %multiply_convert_fusion = bf16[64,16,32,64]{3,0,2,1:T(8,128)(2,1)} fusion(f32[16,32,64]{2,1,0:T(8,128)S(1)} %copy-done.2, bf16[64,64,16,32]{0,3,2,1:T(8,128)(2,1)} %bitcast.38, bf16[64,64]{1,0:T(8,128)(2,1)S(1)} %copy-done.4), kind=kOutput, calls=%fused_computation | convolution fusion | flops 276824064 | bytes 8527872 | tf_op jit(solution)/shard_map/dot_general | solution.py:14
  351.9 12.2 %copy.52 = bf16[64,16,32,64]{3,2,1,0:T(8,128)(2,1)} copy(bf16[64,16,32,64]{3,0,2,1:T(8,128)(2,1)} %multiply_convert_fusion) | data formatting | bytes 8388608 | tf_op jit(solution)/shard_map/convert_element_type | solution.py:15
  (6 shorter events, 0.0 us)
Async XLA Ops:
  0.0 154.6 %copy-start = (bf16[64,64]{1,0:T(8,128)(2,1)S(1)}, bf16[64,64]{1,0:T(8,128)(2,1)}, u32[]{:S(2)}) copy-start(bf16[64,64]{1,0:T(8,128)(2,1)} %param.8) | copy-start | bytes 24580
  248.7 16.3 %copy-start.3 = (bf16[64,64]{1,0:T(8,128)(2,1)S(1)}, bf16[64,64]{1,0:T(8,128)(2,1)}, u32[]{:S(2)}) copy-start(bf16[64,64]{1,0:T(8,128)(2,1)} %param.7) | copy-start | bytes 24580
  320.3 16.4 %copy-start.2 = (f32[16,32,64]{2,1,0:T(8,128)S(1)}, f32[16,32,64]{2,1,0:T(8,128)}, u32[]{:S(2)}) copy-start(f32[16,32,64]{2,1,0:T(8,128)} %param.9) | copy-start | bytes 393220
  320.3 16.4 %copy-start.4 = (bf16[64,64]{1,0:T(8,128)(2,1)S(1)}, bf16[64,64]{1,0:T(8,128)(2,1)}, u32[]{:S(2)}) copy-start(bf16[64,64]{1,0:T(8,128)(2,1)} %param.6) | copy-start | bytes 24580
  336.6 27.5 %copy-start.1 = (bf16[64,64]{1,0:T(8,128)(2,1)S(1)}, bf16[64,64]{1,0:T(8,128)(2,1)}, u32[]{:S(2)}) copy-start(bf16[64,64]{1,0:T(8,128)(2,1)} %param.8) | copy-start | bytes 24580
where the time goes:
time: 371 us; the launch traced here: 364 us
  local copies, waits for them, and re-layouts  207 us (56%)
  blocking collectives  123 us (33%)
  matrix products  34.1 us (9%)
    unnamed x17, local copies, waits for them, and re-layouts  98.8 us
    all_to_all x1, blocking collectives, local_step(): full_three = lax.all_to_all(vol_blk, 'm3', 0, 3, tiled=True)  56.4 us
    all_to_all x1, blocking collectives, local_step(): full_two = lax.all_to_all(prod_three, 'm2', 3, 2, tiled=True)  53.4 us
    all_to_all x2, local copies, waits for them, and re-layouts, local_step(): full_three = lax.all_to_all(vol_blk, 'm3', 0, 3, tiled=True)  38.4 us
    all_to_all x1, local copies, waits for them, and re-layouts, local_step(): full_one = lax.all_to_all(prod_two, 'm1', 3, 1, tiled=True)  16.3 us
    all_to_all x1, local copies, waits for them, and re-layouts, local_step(): full_two = lax.all_to_all(prod_three, 'm2', 3, 2, tiled=True)  16.3 us
    dot_general x1, matrix products, local_step(): lax.dot_general(full_one, fac_one, (((1,), (1,)), ((), ())), preferred_el...  15.3 us
    all_to_all x1, blocking collectives, local_step(): full_one = lax.all_to_all(prod_two, 'm1', 3, 1, tiled=True)  13.2 us

commit v1 on v0

v1 whole, which is shorter than its diff:
```python
import functools

import jax
import jax.numpy as jnp
from jax import lax
from jax.experimental import pallas as pl
from jax.experimental.pallas import tpu as pltpu
from jax.sharding import PartitionSpec as P

MESH = pl.DeviceIdType.MESH
BF16, F32 = jnp.bfloat16, jnp.float32
SG = 8
PIECES = 2
X_PARTS = 4


def dot(lhs, rhs, contract=((1,), (0,))):
    return lax.dot_general(lhs, rhs, (contract, ((), ())), preferred_element_type=F32)


def iota(shape, dim):
    return lax.broadcasted_iota(jnp.int32, shape, dim)


def onehot(cond):
    return jnp.where(cond, 1.0, 0.0).astype(BF16)


def kernel(dims, x_hbm, a1_hbm, a2_hbm, a3_hbm, d_hbm, out, xbuf, tbuf, r1, u3, r2, v2, r3, w1, w2, w3, ident, a1, a2, a3, dbuf,
           in_sem, fac_sem, y_send, y_recv, x_send, x_recv, c_send, c_recv):
    n3, n2, n1, na, nb, nl, ns, nk, nj, ni = dims
    me3, me2, me1 = lax.axis_index("m3"), lax.axis_index("m2"), lax.axis_index("m1")
    groups = ns // n3 // SG
    rows = na * SG
    pairs = na // 2
    ppp = pairs // PIECES
    prow = rows // PIECES
    kb, jb = nk // n2, nj // n1
    bl, bk, kj = nb * nl, nb * kb, kb * jb

    loads = []
    apart = na // X_PARTS
    for h in range(X_PARTS):
        part = pl.ds(h * apart, apart)
        loads.append(pltpu.make_async_copy(x_hbm.at[part], xbuf.at[part], in_sem.at[h]))
        loads[-1].start()
    facs = [pltpu.make_async_copy(s, t, fac_sem.at[i]) for i, (s, t) in enumerate(((a3_hbm, a3), (a2_hbm, a2), (a1_hbm, a1), (d_hbm, dbuf)))]
    for f in facs:
        f.start()

    barrier = pltpu.get_barrier_semaphore()
    peers = 0
    for axis, me, n in (("m3", me3, n3), ("m2", me2, n2), ("m1", me1, n1)):
        for d in range(1, n):
            pl.semaphore_signal(barrier, inc=1, device_id={axis: lax.rem(me + d, n)}, device_id_type=MESH)
            peers += 1

    sd = ns // n3
    r, c = iota((ns, ns), 0), iota((ns, ns), 1)
    want = lax.rem(r // sd + me3, n3) * sd + lax.rem(r, sd)
    ident[...] = onehot(c == want)

    def y_copy(d, g, p):
        at = pl.ds(p * ppp, ppp)
        return pltpu.make_async_remote_copy(
            src_ref=tbuf.at[d, g, at], dst_ref=r1.at[d - 1, g, at], send_sem=y_send.at[d - 1, g * PIECES + p],
            recv_sem=y_recv.at[d - 1, g * PIECES + p], device_id={"m3": lax.rem(me3 + d, n3)}, device_id_type=MESH)

    def x_copy(d, g, p):
        at = pl.ds(p * prow, prow)
        return pltpu.make_async_remote_copy(
            src_ref=u3.at[d, g, at], dst_ref=r2.at[d - 1, g, at], send_sem=x_send.at[d - 1, g * PIECES + p],
            recv_sem=x_recv.at[d - 1, g * PIECES + p], device_id={"m2": lax.rem(me2 + d, n2)}, device_id_type=MESH)

    def c_copy(g):
        return pltpu.make_async_remote_copy(
            src_ref=v2.at[1, g], dst_ref=r3.at[g], send_sem=c_send.at[g], recv_sem=c_recv.at[g],
            device_id={"m1": lax.rem(me1 + 1, n1)}, device_id_type=MESH)

    eye = ident[...]
    per = pairs // X_PARTS
    for h in range(X_PARTS):
        loads[h].wait()

        def turn(i, carry):
            ap = h * per + i
            f0 = dot(eye, xbuf[2 * ap].reshape(bl, ns), ((1,), (1,)))
            f1 = dot(eye, xbuf[2 * ap + 1].reshape(bl, ns), ((1,), (1,)))
            both = jnp.stack([f0.reshape(ns // SG, SG, bl), f1.reshape(ns // SG, SG, bl)], axis=1)
            tbuf[:, :, ap] = both.reshape(n3, groups, 2 * SG, bl).astype(BF16)
            return carry

        lax.fori_loop(0, per, turn, 0)
        if h == 0:
            pl.semaphore_wait(barrier, peers)
        if (h + 1) % (X_PARTS // PIECES) == 0:
            for d in range(1, n3):
                y_copy(d, 0, h // (X_PARTS // PIECES)).start()

    def send_rest(g, carry):
        for p in range(PIECES):
            for d in range(1, n3):
                y_copy(d, g, p).start()
        return carry

    lax.fori_loop(1, groups, send_rest, 0)

    for f in facs:
        f.wait()
    c = iota((nk, n2 * bk), 1)
    pick = onehot(iota((nk, n2 * bk), 0) == lax.rem(c // bk + me2, n2) * kb + lax.rem(c, kb))
    cols3 = dot(a3[...], pick, ((0,), (0,))).astype(BF16)
    r, c = iota((bl, n2 * bk), 0), iota((bl, n2 * bk), 1)
    same_b = r // nl == lax.rem(c // kb, nb)
    for d in range(n3):
        r = iota((bl, n3 * nl), 0)
        sel = onehot(iota((bl, n3 * nl), 1) == lax.rem(me3 - d + n3, n3) * nl + lax.rem(r, nl))
        w1[d * bl : (d + 1) * bl, :] = jnp.where(same_b, dot(sel, cols3), 0.0).astype(BF16)

    c = iota((n2 * nb, n2 * bk), 1)
    pick = onehot(iota((n2 * nb, n2 * bk), 0) == lax.rem(me2 - c // bk + n2, n2) * nb + lax.rem(c // kb, nb))
    cols2 = dot(a2[...], pick).astype(BF16)
    r, c = iota((kj, n2 * bk), 0), iota((kj, n2 * bk), 1)
    same_k = r // jb == lax.rem(c, kb)
    for e in range(n1):
        r = iota((kj, nj), 0)
        sel = onehot(iota((kj, nj), 1) == lax.rem(me1 + e, n1) * jb + lax.rem(r, jb))
        w2[e * kj : (e + 1) * kj, :] = jnp.where(same_k, dot(sel, cols2), 0.0).astype(BF16)

    wide = 2 * ni
    c = iota((ni, SG * wide), 1)
    pick = onehot(iota((ni, SG * wide), 0) == lax.rem(c, wide))
    cols1 = dot(a1[...], pick, ((0,), (0,))).astype(BF16)
    r, c = iota((rows, SG * wide), 0), iota((rows, SG * wide), 1)
    same_s = lax.rem(r, SG) == c // wide
    for e in range(n1):
        r = iota((rows, n1 * na), 0)
        sel = onehot(iota((rows, n1 * na), 1) == lax.rem(me1 + e, n1) * na + r // SG)
        w3[e * rows : (e + 1) * rows, :] = jnp.where(same_s, dot(sel, cols1), 0.0).astype(BF16)

    def stage1(g, p):
        for d in range(1, n3):
            y_copy(d, g, p).wait_recv()
        at = pl.ds(p * ppp, ppp)
        lhs = [tbuf[0, g, at].reshape(prow, bl)] + [r1[d, g, at].reshape(prow, bl) for d in range(n3 - 1)]
        lhs = jnp.concatenate(lhs, axis=1)
        for d in (*range(1, n2), 0):
            u3[d, g, pl.ds(p * prow, prow)] = dot(lhs, w1[:, d * bk : (d + 1) * bk]).astype(BF16)
            if d:
                x_copy(d, g, p).start()

    def stage2(g):
        for p in range(PIECES):
            for d in range(1, n2):
                x_copy(d, g, p).wait_recv()
        rhs = jnp.concatenate([u3[0, g]] + [r2[d, g] for d in range(n2 - 1)], axis=1)
        for e in (1, 0):
            v2[e, g] = dot(w2[e * kj : (e + 1) * kj, :], rhs, ((1,), (1,))).astype(BF16)
            if e:
                c_copy(g).start()

    def stage3(g):
        c_copy(g).wait_recv()
        lhs = jnp.concatenate([v2[0, g], r3[g]], axis=1)
        scale = dbuf[...].reshape(kj, ni)
        for q in range(SG // 2):
            prod = dot(lhs, w3[:, q * 2 * wide : (q + 1) * 2 * wide]).astype(BF16)
            for i in range(2):
                one = prod[:, i * wide : i * wide + ni].astype(F32)
                out[g * SG + 2 * q + i] = (scale * one).astype(BF16).reshape(kb, jb, ni)

    def step(t, carry):
        @pl.when(t < groups)
        def _():
            for p in range(PIECES):
                stage1(t, p)

        @pl.when(jnp.logical_and(t >= 2, t < groups + 2))
        def _():
            stage2(t - 2)

        @pl.when(t >= 3)
        def _():
            stage3(t - 3)

        return carry

    lax.fori_loop(0, groups + 3, step, 0)

    def drain(g, carry):
        for p in range(PIECES):
            for d in range(1, n3):
                y_copy(d, g, p).wait_send()
            for d in range(1, n2):
                x_copy(d, g, p).wait_send()
        c_copy(g).wait_send()
        return carry

    lax.fori_loop(0, groups, drain, 0)


def solution(mesh):
    n3, n2, n1 = mesh.shape["m3"], mesh.shape["m2"], mesh.shape["m1"]

    def local_step(vol_blk, fac_one, fac_two, fac_three, diag_blk):
        ns, na, nb, nl = vol_blk.shape
        nk, nj, ni = fac_three.shape[0], fac_two.shape[0], fac_one.shape[0]
        kb, jb = nk // n2, nj // n1
        groups, rows = ns // n3 // SG, na * SG
        bl, bk, kj = nb * nl, nb * kb, kb * jb
        dims = (n3, n2, n1, na, nb, nl, ns, nk, nj, ni)
        dma = pltpu.SemaphoreType.DMA
        any_space = pl.BlockSpec(memory_space=pl.ANY)
        scratch = [
            pltpu.VMEM((na, nb, nl, ns), BF16),
            pltpu.VMEM((n3, groups, na // 2, 2 * SG, bl), BF16),
            pltpu.VMEM((n3 - 1, groups, na // 2, 2 * SG, bl), BF16),
            pltpu.VMEM((n2, groups, rows, bk), BF16),
            pltpu.VMEM((n2 - 1, groups, rows, bk), BF16),
            pltpu.VMEM((n1, groups, kj, rows), BF16),
            pltpu.VMEM((groups, kj, rows), BF16),
            pltpu.VMEM((n3 * bl, n2 * bk), BF16),
            pltpu.VMEM((n1 * kj, n2 * bk), BF16),
            pltpu.VMEM((n1 * rows, SG * 2 * ni), BF16),
            pltpu.VMEM((ns, ns), BF16),
            pltpu.VMEM(fac_one.shape, BF16),
            pltpu.VMEM(fac_two.shape, BF16),
            pltpu.VMEM(fac_three.shape, BF16),
            pltpu.VMEM(diag_blk.shape, F32),
            dma((X_PARTS,)), dma((4,)),
            dma((n3 - 1, groups * PIECES)), dma((n3 - 1, groups * PIECES)),
            dma((n2 - 1, groups * PIECES)), dma((n2 - 1, groups * PIECES)),
            dma((groups,)), dma((groups,)),
        ]
        call = pl.pallas_call(
            functools.partial(kernel, dims),
            out_shape=pltpu.VMEM((ns // n3, kb, jb, ni), BF16),
            in_specs=[any_space] * 5,
            out_specs=pl.BlockSpec(memory_space=pltpu.VMEM),
            scratch_shapes=scratch,
            compiler_params=pltpu.CompilerParams(collective_id=0, has_side_effects=True, vmem_limit_bytes=50 * 1024 * 1024),
        )
        return call(jnp.transpose(vol_blk, (1, 2, 3, 0)), fac_one, fac_two, fac_three, diag_blk)

    return jax.shard_map(local_step, mesh=mesh, in_specs=(P("dp", "m1", "m2", "m3"), P(), P(), P(), P("m2", "m1", None)), out_specs=P(("dp", "m3"), "m2", "m1", None), check_vma=False)
```

time: 371 us -> 70.7 us (0.19); the launches traced: 364 us -> 70.6 us
  local copies, waits for them, and re-layouts: 207 us -> 3.4 us
  blocking collectives: 123 us -> 0 us
  Pallas kernels: 0 us -> 67.2 us
  matrix products: 34.1 us -> 0 us
    all_to_all x3 -> x0, blocking collectives: 123 us -> none  [the longest x1 56.4 us: local_step(): full_three = lax.all_to_all(vol_blk, 'm3', 0, 3, tiled=True)]
    unnamed x17 -> x1, local copies, waits for them, and re-layouts: 98.8 us -> 3.4 us
    all_to_all x4 -> x0, local copies, waits for them, and re-layouts: 71 us -> none  [the longest x2 38.4 us: local_step(): full_three = lax.all_to_all(vol_blk, 'm3', 0, 3, tiled=True)]
    pallas_call x0 -> x1, Pallas kernels: none -> 67.2 us  [local_step(): call(jnp.transpose(vol_blk, (1, 2, 3, 0)), fac_one, fac_two, fac_three, d...]
    convert_element_type x3 -> x0, local copies, waits for them, and re-layouts: 37.2 us -> none  [the longest x1 12.5 us: local_step(): lax.dot_general(full_three, fac_three, (((3,), (1,)), ((), ())), preferre...]
    dot_general x3 -> x0, matrix products: 34.1 us -> none  [the longest x1 15.3 us: local_step(): lax.dot_general(full_one, fac_one, (((1,), (1,)), ((), ())), preferred_el...]
where the time goes in v1:
time: 70.7 us; the launch traced here: 70.6 us
  Pallas kernels  67.2 us (95%)
  local copies, waits for them, and re-layouts  3.4 us (5%)
    pallas_call x1, Pallas kernels, local_step(): call(jnp.transpose(vol_blk, (1, 2, 3, 0)), fac_one, fac_two, fac_three, d...  67.2 us
    unnamed x1, local copies, waits for them, and re-layouts  3.4 us

profile of v1, /device:TPU:97, one launch (start us, length us, event | category | flops | bytes accessed | tf_op | source)
XLA Modules:
  0.0 70.6 jit_solution(15389315197777515063)
XLA Ops:
  0.0 67.2 %shard_map.55 = bf16[64,16,32,64]{3,2,1,0:T(8,128)(2,1)S(1)} custom-call(bf16[32,16,16,256]{3,2,1,0:T(8,128)(2,1)} %bitcast.1, bf16[64,64]{1,0:T(8,128)(2,1)} %a1_hbm.1, bf16[64,64]{1,0:T(8,128)(2,1)} %a2_hbm.1, bf16[64,64]{1,0:T(8,128)(2,1)} %a3_hbm.1, f32[16,32,64]{2,1,0:T(8,128)} %d_hbm.1), custom_call_target="tpu_custom_call" | custom-call | tf_op jit(solution)/shard_map/pallas_call | solution.py:243
  67.2 3.4 %copy.7 = bf16[64,16,32,64]{3,2,1,0:T(8,128)(2,1)} copy(bf16[64,16,32,64]{3,2,1,0:T(8,128)(2,1)S(1)} %shard_map.55) | data formatting | bytes 8388608

commit v2 on v0

v2 whole, which is shorter than its diff:
```python
import functools

import jax
import jax.numpy as jnp
from jax import lax
from jax.experimental import pallas as pl
from jax.experimental.pallas import tpu as pltpu
from jax.sharding import PartitionSpec as P

MESH = pl.DeviceIdType.MESH
BF16, F32 = jnp.bfloat16, jnp.float32
SG = 8
PIECES = 4
AHEAD = 3
LANES = 128


def far_first(n):
    return sorted(range(1, n), key=lambda d: -min(d, n - d))


def dot(lhs, rhs, contract=((1,), (0,))):
    return lax.dot_general(lhs, rhs, (contract, ((), ())), preferred_element_type=F32)


def iota(shape, dim):
    return lax.broadcasted_iota(jnp.int32, shape, dim)


def onehot(cond):
    return jnp.where(cond, 1.0, 0.0).astype(BF16)


def kernel(dims, x_hbm, a1_hbm, a2_hbm, a3_hbm, d_hbm, out, xbuf, tbuf, r1, u3, r2, v2, r3, w1, w2, w3, ident, a1, a2, a3, dbuf,
           in_sem, fac_sem, y_send, y_recv, x_send, x_recv, c_send, c_recv):
    n3, n2, n1, na, nb, nl, ns, nk, nj, ni = dims
    me3, me2, me1 = lax.axis_index("m3"), lax.axis_index("m2"), lax.axis_index("m1")
    groups = ns // n3 // SG
    rows = na * SG
    pairs = na // 2
    ppp = pairs // PIECES
    prow = rows // PIECES
    kb, jb = nk // n2, nj // n1
    bl, bk, kj = nb * nl, nb * kb, kb * jb
    bt, kt = bl // LANES, bk // LANES
    bs, ks = nb // bt, kb // kt
    half = ks * jb

    facs = [pltpu.make_async_copy(s, t, fac_sem.at[i]) for i, (s, t) in enumerate(((a3_hbm, a3), (a2_hbm, a2), (a1_hbm, a1), (d_hbm, dbuf)))]
    facs[0].start()
    loads = []
    apart = na // PIECES
    for h in range(PIECES):
        part = pl.ds(h * apart, apart)
        loads.append(pltpu.make_async_copy(x_hbm.at[part], xbuf.at[part], in_sem.at[h]))
        loads[-1].start()
    for f in facs[1:]:
        f.start()

    barrier = pltpu.get_barrier_semaphore()
    peers = 0
    for axis, me, n in (("m3", me3, n3), ("m2", me2, n2), ("m1", me1, n1)):
        for d in range(1, n):
            pl.semaphore_signal(barrier, inc=1, device_id={axis: lax.rem(me + d, n)}, device_id_type=MESH)
            peers += 1

    def y_copy(src, dst, sem, d=1):
        return pltpu.make_async_remote_copy(src_ref=src, dst_ref=dst, send_sem=y_send, recv_sem=y_recv.at[sem],
                                            device_id={"m3": lax.rem(me3 + d, n3)}, device_id_type=MESH)

    def x_copy(src, dst, sem, d=1):
        return pltpu.make_async_remote_copy(src_ref=src, dst_ref=dst, send_sem=x_send, recv_sem=x_recv.at[sem],
                                            device_id={"m2": lax.rem(me2 + d, n2)}, device_id_type=MESH)

    def c_copy(src, dst, sem):
        return pltpu.make_async_remote_copy(src_ref=src, dst_ref=dst, send_sem=c_send, recv_sem=c_recv.at[sem],
                                            device_id={"m1": lax.rem(me1 + 1, n1)}, device_id_type=MESH)

    def send_piece(g, p):
        at = pl.ds(p * ppp, ppp)
        for d in far_first(n3):
            y_copy(tbuf.at[d, g, at], r1.at[d - 1, g, at], g * PIECES + p, d).start()

    def send_group(g):
        for p in range(PIECES):
            send_piece(g, p)

    sd = ns // n3
    r, c = iota((ns, ns), 0), iota((ns, ns), 1)
    ident[...] = onehot(c == lax.rem(r // sd + me3, n3) * sd + lax.rem(r, sd))

    c = iota((nk, n2 * LANES), 1)
    k_of = lax.rem(c, LANES) // (LANES // kt) * ks + lax.rem(c, ks)
    pick = onehot(iota((nk, n2 * LANES), 0) == lax.rem(c // LANES + me2, n2) * kb + k_of)
    r, c = iota((LANES, n2 * LANES), 0), iota((LANES, n2 * LANES), 1)
    same_b = r // nl == lax.rem(c // ks, bs)
    facs[0].wait()
    cols3 = dot(a3[...], pick, ((0,), (0,))).astype(BF16)
    for d in range(n3):
        r = iota((LANES, n3 * nl), 0)
        sel = onehot(iota((LANES, n3 * nl), 1) == lax.rem(me3 - d + n3, n3) * nl + lax.rem(r, nl))
        w1[d * LANES : (d + 1) * LANES, :] = jnp.where(same_b, dot(sel, cols3), 0.0).astype(BF16)

    def build_rest():
        for f in facs[1:]:
            f.wait()
        c = iota((n2 * nb, n2 * LANES), 1)
        pick = onehot(iota((n2 * nb, n2 * LANES), 0) == lax.rem(me2 - c // LANES + n2, n2) * nb + lax.rem(c, LANES) // ks)
        cols2 = dot(a2[...], pick).astype(BF16)
        r, c = iota((half, n2 * LANES), 0), iota((half, n2 * LANES), 1)
        same_k = r // jb == lax.rem(c, ks)
        for e in range(n1):
            r = iota((half, nj), 0)
            sel = onehot(iota((half, nj), 1) == lax.rem(me1 + e, n1) * jb + lax.rem(r, jb))
            w2[e * half : (e + 1) * half, :] = jnp.where(same_k, dot(sel, cols2), 0.0).astype(BF16)

        c = iota((ni, SG * wide), 1)
        pick = onehot(iota((ni, SG * wide), 0) == lax.rem(c, wide))
        cols1 = dot(a1[...], pick, ((0,), (0,))).astype(BF16)
        r, c = iota((rows, SG * wide), 0), iota((rows, SG * wide), 1)
        same_s = lax.rem(r, SG) == c // wide
        for e in range(n1):
            r = iota((rows, n1 * na), 0)
            sel = onehot(iota((rows, n1 * na), 1) == lax.rem(me1 + e, n1) * na + r // SG)
            w3[e * rows : (e + 1) * rows, :] = jnp.where(same_s, dot(sel, cols1), 0.0).astype(BF16)

    wide = 2 * ni
    eye = ident[...]
    for h in range(PIECES):
        loads[h].wait()
        for ap in range(h * ppp, (h + 1) * ppp):
            two = [dot(eye, xbuf[2 * ap + i].reshape(bl, ns), ((1,), (1,))).reshape(ns // SG, SG, bl) for i in range(2)]
            tbuf[:, :, ap] = jnp.stack(two, axis=1).reshape(n3, groups, 2 * SG, bl).astype(BF16)
        if h == 0:
            pl.semaphore_wait(barrier, peers)
        send_piece(0, h)
    for g in range(1, AHEAD):
        send_group(g)

    def stage1(g, p):
        at = pl.ds(p * ppp, ppp)
        y_copy(tbuf.at[pl.ds(1, n3 - 1), g, at], r1.at[:, g, at], g * PIECES + p).wait_recv()
        got = [tbuf[0, g, at].reshape(prow, bl)] + [r1[d, g, at].reshape(prow, bl) for d in range(n3 - 1)]
        lhs = [jnp.concatenate([v[:, t * LANES : (t + 1) * LANES] for v in got], axis=1) for t in range(bt)]
        prod = dot(jnp.concatenate(lhs, axis=0), w1[...])
        width = LANES // bt
        slot = iota((prow, LANES), 1) // width
        at = pl.ds(p * prow, prow)
        for d in (*far_first(n2), 0):
            by_b = [prod[t * prow : (t + 1) * prow, d * LANES : (d + 1) * LANES] for t in range(bt)]
            for u in range(kt):
                tile = by_b[u]
                for t in range(bt):
                    if t != u:
                        tile = jnp.where(slot == t, pltpu.roll(by_b[t], (t - u) * width % LANES, 1), tile)
                u3[d, g, at, u * LANES : (u + 1) * LANES] = tile.astype(BF16)
            if d:
                x_copy(u3.at[d, g, at], r2.at[d - 1, g, at], g, d).start()

    def stage2(g):
        x_copy(u3.at[pl.ds(1, n2 - 1), g], r2.at[:, g], g).wait_recv()
        got = [u3.at[0, g]] + [r2.at[d, g] for d in range(n2 - 1)]
        for u in range(kt):
            rhs = jnp.concatenate([v[:, u * LANES : (u + 1) * LANES] for v in got], axis=1)
            prod = dot(w2[...], rhs, ((1,), (1,))).astype(BF16)
            at = pl.ds(u * half, half)
            for e in range(n1 - 1, -1, -1):
                v2[e, g, at] = prod[e * half : (e + 1) * half, :]
            c_copy(v2.at[1, g, at], r3.at[g, at], g).start()

    def stage3(g):
        c_copy(v2.at[1, g], r3.at[g], g).wait_recv()
        lhs = jnp.concatenate([v2[0, g], r3[g]], axis=1)
        scale = dbuf[...].reshape(kj, ni)
        for q in range(SG // 2):
            prod = dot(lhs, w3[:, q * 2 * wide : (q + 1) * 2 * wide]).astype(BF16)
            for i in range(2):
                one = prod[:, i * wide : i * wide + ni].astype(F32)
                out[g * SG + 2 * q + i] = (scale * one).astype(BF16).reshape(kb, jb, ni)

    def step(g, carry):
        for p in range(PIECES):
            stage1(g, p)
            if p == PIECES - 2:
                pl.when(g >= 2)(lambda: stage3(g - 2))
        pl.when(g + AHEAD < groups)(lambda: send_group(g + AHEAD))
        pl.when(g == 0)(build_rest)
        pl.when(g >= 1)(lambda: stage2(g - 1))
        return carry

    lax.fori_loop(0, groups, step, 0)
    stage3(groups - 2)
    stage2(groups - 1)
    stage3(groups - 1)

    y_copy(tbuf.at[pl.ds(1, n3 - 1)], r1, 0).wait_send()
    x_copy(u3.at[pl.ds(1, n2 - 1)], r2, 0).wait_send()
    c_copy(v2.at[1], r3, 0).wait_send()


def solution(mesh):
    n3, n2, n1 = mesh.shape["m3"], mesh.shape["m2"], mesh.shape["m1"]

    def local_step(vol_blk, fac_one, fac_two, fac_three, diag_blk):
        ns, na, nb, nl = vol_blk.shape
        nk, nj, ni = fac_three.shape[0], fac_two.shape[0], fac_one.shape[0]
        kb, jb = nk // n2, nj // n1
        groups, rows = ns // n3 // SG, na * SG
        bl, bk, kj = nb * nl, nb * kb, kb * jb
        dims = (n3, n2, n1, na, nb, nl, ns, nk, nj, ni)
        dma = pltpu.SemaphoreType.DMA
        any_space = pl.BlockSpec(memory_space=pl.ANY)
        scratch = [
            pltpu.VMEM((na, nb, nl, ns), BF16),
            pltpu.VMEM((n3, groups, na // 2, 2 * SG, bl), BF16),
            pltpu.VMEM((n3 - 1, groups, na // 2, 2 * SG, bl), BF16),
            pltpu.VMEM((n2, groups, rows, bk), BF16),
            pltpu.VMEM((n2 - 1, groups, rows, bk), BF16),
            pltpu.VMEM((n1, groups, kj, rows), BF16),
            pltpu.VMEM((groups, kj, rows), BF16),
            pltpu.VMEM((n3 * LANES, n2 * LANES), BF16),
            pltpu.VMEM((n1 * kj * LANES // bk, n2 * LANES), BF16),
            pltpu.VMEM((n1 * rows, SG * 2 * ni), BF16),
            pltpu.VMEM((ns, ns), BF16),
            pltpu.VMEM(fac_one.shape, BF16),
            pltpu.VMEM(fac_two.shape, BF16),
            pltpu.VMEM(fac_three.shape, BF16),
            pltpu.VMEM(diag_blk.shape, F32),
            dma((PIECES,)), dma((4,)), dma, dma((groups * PIECES,)), dma, dma((groups,)), dma, dma((groups,)),
        ]
        call = pl.pallas_call(
            functools.partial(kernel, dims),
            out_shape=pltpu.VMEM((ns // n3, kb, jb, ni), BF16),
            in_specs=[any_space] * 5,
            out_specs=pl.BlockSpec(memory_space=pltpu.VMEM),
            scratch_shapes=scratch,
            compiler_params=pltpu.CompilerParams(collective_id=0, has_side_effects=True, vmem_limit_bytes=50 * 1024 * 1024),
        )
        return call(jnp.transpose(vol_blk, (1, 2, 3, 0)), fac_one, fac_two, fac_three, diag_blk)

    return jax.shard_map(local_step, mesh=mesh, in_specs=(P("dp", "m1", "m2", "m3"), P(), P(), P(), P("m2", "m1", None)), out_specs=P(("dp", "m3"), "m2", "m1", None), check_vma=False)
```

time: 371 us -> 66.4 us (0.18); the launches traced: 364 us -> 66.3 us
  local copies, waits for them, and re-layouts: 207 us -> 3.4 us
  blocking collectives: 123 us -> 0 us
  Pallas kernels: 0 us -> 62.9 us
  matrix products: 34.1 us -> 0 us
    all_to_all x3 -> x0, blocking collectives: 123 us -> none  [the longest x1 56.4 us: local_step(): full_three = lax.all_to_all(vol_blk, 'm3', 0, 3, tiled=True)]
    unnamed x17 -> x1, local copies, waits for them, and re-layouts: 98.8 us -> 3.4 us
    all_to_all x4 -> x0, local copies, waits for them, and re-layouts: 71 us -> none  [the longest x2 38.4 us: local_step(): full_three = lax.all_to_all(vol_blk, 'm3', 0, 3, tiled=True)]
    pallas_call x0 -> x1, Pallas kernels: none -> 62.9 us  [local_step(): call(jnp.transpose(vol_blk, (1, 2, 3, 0)), fac_one, fac_two, fac_three, d...]
    convert_element_type x3 -> x0, local copies, waits for them, and re-layouts: 37.2 us -> none  [the longest x1 12.5 us: local_step(): lax.dot_general(full_three, fac_three, (((3,), (1,)), ((), ())), preferre...]
    dot_general x3 -> x0, matrix products: 34.1 us -> none  [the longest x1 15.3 us: local_step(): lax.dot_general(full_one, fac_one, (((1,), (1,)), ((), ())), preferred_el...]
where the time goes in v2:
time: 66.4 us; the launch traced here: 66.3 us
  Pallas kernels  62.9 us (95%)
  local copies, waits for them, and re-layouts  3.4 us (5%)
    pallas_call x1, Pallas kernels, local_step(): call(jnp.transpose(vol_blk, (1, 2, 3, 0)), fac_one, fac_two, fac_three, d...  62.9 us
    unnamed x1, local copies, waits for them, and re-layouts  3.4 us

profile of v2, /device:TPU:97, one launch (start us, length us, event | category | flops | bytes accessed | tf_op | source)
XLA Modules:
  0.0 66.3 jit_solution(3710282606729251225)
XLA Ops:
  0.0 62.9 %shard_map.55 = bf16[64,16,32,64]{3,2,1,0:T(8,128)(2,1)S(1)} custom-call(bf16[32,16,16,256]{3,2,1,0:T(8,128)(2,1)} %bitcast.1, bf16[64,64]{1,0:T(8,128)(2,1)} %a1_hbm.1, bf16[64,64]{1,0:T(8,128)(2,1)} %a2_hbm.1, bf16[64,64]{1,0:T(8,128)(2,1)} %a3_hbm.1, f32[16,32,64]{2,1,0:T(8,128)} %d_hbm.1), custom_call_target="tpu_custom_call" | custom-call | tf_op jit(solution)/shard_map/pallas_call | solution.py:239
  62.9 3.4 %copy.7 = bf16[64,16,32,64]{3,2,1,0:T(8,128)(2,1)} copy(bf16[64,16,32,64]{3,2,1,0:T(8,128)(2,1)S(1)} %shard_map.55) | data formatting | bytes 8388608

commit v3 on v2

--- a/solution.py
+++ b/solution.py
@@ -11,6 +11,8 @@
 BF16, F32 = jnp.bfloat16, jnp.float32
 SG = 8
 PIECES = 4
+FIRST = (2, 2, 4, 4, 4)
+COPIES = 7
 AHEAD = 3
 LANES = 128
 
@@ -31,7 +33,31 @@
     return jnp.where(cond, 1.0, 0.0).astype(BF16)
 
 
-def kernel(dims, x_hbm, a1_hbm, a2_hbm, a3_hbm, d_hbm, out, xbuf, tbuf, r1, u3, r2, v2, r3, w1, w2, w3, ident, a1, a2, a3, dbuf,
+def third(lhs, w3, d_ref, out, base, shape):
+    ni = shape[-1]
+    wide = w3.shape[1] // SG
+    scale = d_ref[...].reshape(-1, ni)
+    for q in range(SG // 2):
+        prod = dot(lhs, w3[:, q * 2 * wide : (q + 1) * 2 * wide]).astype(BF16)
+        for i in range(2):
+            one = prod[:, i * wide : i * wide + ni].astype(F32)
+            out[base + 2 * q + i] = (scale * one).astype(BF16).reshape(shape)
+
+
+def finish(done, last, w3, d_ref, out, tail, sem):
+    size = done.shape[0]
+    chunk = size // COPIES
+    copies = [pltpu.make_async_copy(done.at[pl.ds(i * chunk, chunk)], out.at[pl.ds(i * chunk, chunk)], sem.at[i]) for i in range(COPIES)]
+    for c in copies:
+        c.start()
+    third(last[...], w3, d_ref, tail, 0, tail.shape[1:])
+    copies.append(pltpu.make_async_copy(tail, out.at[pl.ds(size, SG)], sem.at[COPIES]))
+    copies[-1].start()
+    for c in copies:
+        c.wait()
+
+
+def kernel(dims, x_hbm, a1_hbm, a2_hbm, a3_hbm, d_hbm, out, last, w3, dbuf, xbuf, tbuf, r1, u3, r2, v2, r3, w1, w2, ident, a1, a2, a3,
            in_sem, fac_sem, y_send, y_recv, x_send, x_recv, c_send, c_recv):
     n3, n2, n1, na, nb, nl, ns, nk, nj, ni = dims
     me3, me2, me1 = lax.axis_index("m3"), lax.axis_index("m2"), lax.axis_index("m1")
@@ -46,16 +72,13 @@
     bs, ks = nb // bt, kb // kt
     half = ks * jb
 
+    loads, cuts = [], [0]
+    for n in FIRST:
+        part = pl.ds(2 * cuts[-1], 2 * n)
+        loads.append(pltpu.make_async_copy(x_hbm.at[part], xbuf.at[part], in_sem.at[len(loads)]))
+        cuts.append(cuts[-1] + n)
     facs = [pltpu.make_async_copy(s, t, fac_sem.at[i]) for i, (s, t) in enumerate(((a3_hbm, a3), (a2_hbm, a2), (a1_hbm, a1), (d_hbm, dbuf)))]
-    facs[0].start()
-    loads = []
-    apart = na // PIECES
-    for h in range(PIECES):
-        part = pl.ds(h * apart, apart)
-        loads.append(pltpu.make_async_copy(x_hbm.at[part], xbuf.at[part], in_sem.at[h]))
-        loads[-1].start()
-    for f in facs[1:]:
-        f.start()
+    loads[0].start()
 
     barrier = pltpu.get_barrier_semaphore()
     peers = 0
@@ -63,6 +86,8 @@
         for d in range(1, n):
             pl.semaphore_signal(barrier, inc=1, device_id={axis: lax.rem(me + d, n)}, device_id_type=MESH)
             peers += 1
+    for f in loads[1:] + facs:
+        f.start()
 
     def y_copy(src, dst, sem, d=1):
         return pltpu.make_async_remote_copy(src_ref=src, dst_ref=dst, send_sem=y_send, recv_sem=y_recv.at[sem],
@@ -76,30 +101,18 @@
         return pltpu.make_async_remote_copy(src_ref=src, dst_ref=dst, send_sem=c_send, recv_sem=c_recv.at[sem],
                                             device_id={"m1": lax.rem(me1 + 1, n1)}, device_id_type=MESH)
 
-    def send_piece(g, p):
-        at = pl.ds(p * ppp, ppp)
+    def send_pairs(g, lo, n):
+        at = pl.ds(lo, n)
         for d in far_first(n3):
-            y_copy(tbuf.at[d, g, at], r1.at[d - 1, g, at], g * PIECES + p, d).start()
+            y_copy(tbuf.at[d, g, at], r1.at[d - 1, g, at], g * PIECES + lo // ppp, d).start()
 
     def send_group(g):
         for p in range(PIECES):
-            send_piece(g, p)
+            send_pairs(g, p * ppp, ppp)
 
     sd = ns // n3
     r, c = iota((ns, ns), 0), iota((ns, ns), 1)
     ident[...] = onehot(c == lax.rem(r // sd + me3, n3) * sd + lax.rem(r, sd))
-
-    c = iota((nk, n2 * LANES), 1)
-    k_of = lax.rem(c, LANES) // (LANES // kt) * ks + lax.rem(c, ks)
-    pick = onehot(iota((nk, n2 * LANES), 0) == lax.rem(c // LANES + me2, n2) * kb + k_of)
-    r, c = iota((LANES, n2 * LANES), 0), iota((LANES, n2 * LANES), 1)
-    same_b = r // nl == lax.rem(c // ks, bs)
-    facs[0].wait()
-    cols3 = dot(a3[...], pick, ((0,), (0,))).astype(BF16)
-    for d in range(n3):
-        r = iota((LANES, n3 * nl), 0)
-        sel = onehot(iota((LANES, n3 * nl), 1) == lax.rem(me3 - d + n3, n3) * nl + lax.rem(r, nl))
-        w1[d * LANES : (d + 1) * LANES, :] = jnp.where(same_b, dot(sel, cols3), 0.0).astype(BF16)
 
     def build_rest():
         for f in facs[1:]:
@@ -126,14 +139,27 @@
 
     wide = 2 * ni
     eye = ident[...]
-    for h in range(PIECES):
+    for h, n in enumerate(FIRST):
         loads[h].wait()
-        for ap in range(h * ppp, (h + 1) * ppp):
+        for ap in range(cuts[h], cuts[h + 1]):
             two = [dot(eye, xbuf[2 * ap + i].reshape(bl, ns), ((1,), (1,))).reshape(ns // SG, SG, bl) for i in range(2)]
             tbuf[:, :, ap] = jnp.stack(two, axis=1).reshape(n3, groups, 2 * SG, bl).astype(BF16)
         if h == 0:
             pl.semaphore_wait(barrier, peers)
-        send_piece(0, h)
+        send_pairs(0, cuts[h], n)
+
+    c = iota((nk, n2 * LANES), 1)
+    k_of = lax.rem(c, LANES) // (LANES // kt) * ks + lax.rem(c, ks)
+    pick = onehot(iota((nk, n2 * LANES), 0) == lax.rem(c // LANES + me2, n2) * kb + k_of)
+    r, c = iota((LANES, n2 * LANES), 0), iota((LANES, n2 * LANES), 1)
+    same_b = r // nl == lax.rem(c // ks, bs)
+    facs[0].wait()
+    cols3 = dot(a3[...], pick, ((0,), (0,))).astype(BF16)
+    for d in range(n3):
+        r = iota((LANES, n3 * nl), 0)
+        sel = onehot(iota((LANES, n3 * nl), 1) == lax.rem(me3 - d + n3, n3) * nl + lax.rem(r, nl))
+        w1[d * LANES : (d + 1) * LANES, :] = jnp.where(same_b, dot(sel, cols3), 0.0).astype(BF16)
+
     for g in range(1, AHEAD):
         send_group(g)
 
@@ -157,26 +183,25 @@
             if d:
                 x_copy(u3.at[d, g, at], r2.at[d - 1, g, at], g, d).start()
 
-    def stage2(g):
+    def stage2(g, final=False):
         x_copy(u3.at[pl.ds(1, n2 - 1), g], r2.at[:, g], g).wait_recv()
         got = [u3.at[0, g]] + [r2.at[d, g] for d in range(n2 - 1)]
-        for u in range(kt):
-            rhs = jnp.concatenate([v[:, u * LANES : (u + 1) * LANES] for v in got], axis=1)
-            prod = dot(w2[...], rhs, ((1,), (1,))).astype(BF16)
-            at = pl.ds(u * half, half)
-            for e in range(n1 - 1, -1, -1):
-                v2[e, g, at] = prod[e * half : (e + 1) * half, :]
-            c_copy(v2.at[1, g, at], r3.at[g, at], g).start()
+        for es in ((1,), (0,)) if final else (tuple(range(n1)),):
+            for u in range(kt):
+                rhs = jnp.concatenate([v[:, u * LANES : (u + 1) * LANES] for v in got], axis=1)
+                prod = dot(w2[es[0] * half : (es[-1] + 1) * half, :], rhs, ((1,), (1,))).astype(BF16)
+                at = pl.ds(u * half, half)
+                for k, e in enumerate(es):
+                    if final and e == 0:
+                        last[at, :rows] = prod
+                    else:
+                        v2[e, g, at] = prod[k * half : (k + 1) * half, :]
+                if 1 in es:
+                    c_copy(v2.at[1, g, at], r3.at[g, at], g).start()
 
     def stage3(g):
         c_copy(v2.at[1, g], r3.at[g], g).wait_recv()
-        lhs = jnp.concatenate([v2[0, g], r3[g]], axis=1)
-        scale = dbuf[...].reshape(kj, ni)
-        for q in range(SG // 2):
-            prod = dot(lhs, w3[:, q * 2 * wide : (q + 1) * 2 * wide]).astype(BF16)
-            for i in range(2):
-                one = prod[:, i * wide : i * wide + ni].astype(F32)
-                out[g * SG + 2 * q + i] = (scale * one).astype(BF16).reshape(kb, jb, ni)
+        third(jnp.concatenate([v2[0, g], r3[g]], axis=1), w3, dbuf, out, g * SG, (kb, jb, ni))
 
     def step(g, carry):
         for p in range(PIECES):
@@ -190,8 +215,9 @@
 
     lax.fori_loop(0, groups, step, 0)
     stage3(groups - 2)
-    stage2(groups - 1)
-    stage3(groups - 1)
+    stage2(groups - 1, True)
+    c_copy(v2.at[1, groups - 1], r3.at[groups - 1], groups - 1).wait_recv()
+    last[:, rows:] = r3[groups - 1]
 
     y_copy(tbuf.at[pl.ds(1, n3 - 1)], r1, 0).wait_send()
     x_copy(u3.at[pl.ds(1, n2 - 1)], r2, 0).wait_send()
@@ -220,22 +246,33 @@
             pltpu.VMEM((groups, kj, rows), BF16),
             pltpu.VMEM((n3 * LANES, n2 * LANES), BF16),
             pltpu.VMEM((n1 * kj * LANES // bk, n2 * LANES), BF16),
-            pltpu.VMEM((n1 * rows, SG * 2 * ni), BF16),
             pltpu.VMEM((ns, ns), BF16),
             pltpu.VMEM(fac_one.shape, BF16),
             pltpu.VMEM(fac_two.shape, BF16),
             pltpu.VMEM(fac_three.shape, BF16),
-            pltpu.VMEM(diag_blk.shape, F32),
-            dma((PIECES,)), dma((4,)), dma, dma((groups * PIECES,)), dma, dma((groups,)), dma, dma((groups,)),
+            dma((len(FIRST),)), dma((4,)), dma, dma((groups * PIECES,)), dma, dma((groups,)), dma, dma((groups,)),
         ]
-        call = pl.pallas_call(
+        vmem = pl.BlockSpec(memory_space=pltpu.VMEM)
+        held = pl.pallas_call(
             functools.partial(kernel, dims),
-            out_shape=pltpu.VMEM((ns // n3, kb, jb, ni), BF16),
+            out_shape=(
+                pltpu.VMEM((ns // n3 - SG, kb, jb, ni), BF16),
+                pltpu.VMEM((kj, n1 * rows), BF16),
+                pltpu.VMEM((n1 * rows, SG * 2 * ni), BF16),
+                pltpu.VMEM(diag_blk.shape, F32),
+            ),
             in_specs=[any_space] * 5,
-            out_specs=pl.BlockSpec(memory_space=pltpu.VMEM),
+            out_specs=(vmem,) * 4,
             scratch_shapes=scratch,
             compiler_params=pltpu.CompilerParams(collective_id=0, has_side_effects=True, vmem_limit_bytes=50 * 1024 * 1024),
-        )
-        return call(jnp.transpose(vol_blk, (1, 2, 3, 0)), fac_one, fac_two, fac_three, diag_blk)
+        )(jnp.transpose(vol_blk, (1, 2, 3, 0)), fac_one, fac_two, fac_three, diag_blk)
+        return pl.pallas_call(
+            finish,
+            out_shape=jax.ShapeDtypeStruct((ns // n3, kb, jb, ni), BF16),
+            in_specs=[vmem] * 4,
+            out_specs=any_space,
+            scratch_shapes=[pltpu.VMEM((SG, kb, jb, ni), BF16), dma((COPIES + 1,))],
+            compiler_params=pltpu.CompilerParams(vmem_limit_bytes=12 * 1024 * 1024),
+        )(*held)
 
     return jax.shard_map(local_step, mesh=mesh, in_specs=(P("dp", "m1", "m2", "m3"), P(), P(), P(), P("m2", "m1", None)), out_specs=P(("dp", "m3"), "m2", "m1", None), check_vma=False)

time: 66.4 us -> 65.1 us (0.980)
  local copies, waits for them, and re-layouts: 3.4 us -> 0 us
  Pallas kernels: 62.9 us -> 65 us
    unnamed x1 -> x0, local copies, waits for them, and re-layouts: 3.4 us -> none
    pallas_call x1 -> x2, Pallas kernels: 62.9 us -> 65 us  [the longest x1 61.6 us: local_step(): pl.pallas_call(functools.partial(kernel, dims), out_shape=(pltpu.VMEM((ns...]
where the time goes in v3:
time: 65.1 us; the launch traced here: 65 us
  Pallas kernels  65 us (100%)
    pallas_call x1, Pallas kernels, local_step(): pl.pallas_call(functools.partial(kernel, dims), out_shape=(pltpu.VMEM((ns...  61.6 us
    pallas_call x1, Pallas kernels, local_step(): pl.pallas_call(finish, out_shape=jax.ShapeDtypeStruct((ns // n3, kb, jb,...  3.37 us

profile of v3, /device:TPU:97, one launch (start us, length us, event | category | flops | bytes accessed | tf_op | source)
XLA Modules:
  0.0 65.0 jit_solution(17151597589922170556)
XLA Ops:
  0.0 61.6 %shard_map.55 = (bf16[56,16,32,64]{3,2,1,0:T(8,128)(2,1)S(1)}, bf16[512,512]{1,0:T(8,128)(2,1)S(1)}, bf16[512,1024]{1,0:T(8,128)(2,1)S(1)}, f32[16,32,64]{2,1,0:T(8,128)S(1)}) custom-call(bf16[32,16,16,256]{3,2,1,0:T(8,128)(2,1)} %bitcast.1, bf16[64,64]{1,0:T(8,128)(2,1)} %a1_hbm.1, bf16[64,64]{1,0:T(8,128)(2,1)} %a2_hbm.1, bf16[64,64]{1,0:T(8,128)(2,1)} %a3_hbm.1, ...), custom_call_target="tpu_custom_call" | custom-call | tf_op jit(solution)/shard_map/pallas_call | solution.py:256
  61.6 3.4 %shard_map.56 = bf16[64,16,32,64]{3,2,1,0:T(8,128)(2,1)} custom-call(bf16[56,16,32,64]{3,2,1,0:T(8,128)(2,1)S(1)} %get-tuple-element.9.done, bf16[512,512]{1,0:T(8,128)(2,1)S(1)} %get-tuple-element.10.last, bf16[512,1024]{1,0:T(8,128)(2,1)S(1)} %get-tuple-element.11.w3, f32[16,32,64]{2,1,0:T(8,128)S(1)} %get-tuple-element.12.d_ref), custom_call_target="tpu_custom_call" | custom-call | tf_op jit(solution)/shard_map/pallas_call | solution.py:269

commit v4 on v3

--- a/solution.py
+++ b/solution.py
@@ -10,10 +10,12 @@
 MESH = pl.DeviceIdType.MESH
 BF16, F32 = jnp.bfloat16, jnp.float32
 SG = 8
-PIECES = 4
-FIRST = (2, 2, 4, 4, 4)
+PIECES = 8
+FIRST = (1, 1) + (2,) * 7
 COPIES = 7
-AHEAD = 3
+FIRST_SEND_AT = 0
+SEND_AT, THIRD_AT = (2,), (3,)
+AHEAD = 2
 LANES = 128
 
 
@@ -33,11 +35,11 @@
     return jnp.where(cond, 1.0, 0.0).astype(BF16)
 
 
-def third(lhs, w3, d_ref, out, base, shape):
+def third(lhs, w3, d_ref, out, base, shape, pairs=range(SG // 2)):
     ni = shape[-1]
     wide = w3.shape[1] // SG
     scale = d_ref[...].reshape(-1, ni)
-    for q in range(SG // 2):
+    for q in pairs:
         prod = dot(lhs, w3[:, q * 2 * wide : (q + 1) * 2 * wide]).astype(BF16)
         for i in range(2):
             one = prod[:, i * wide : i * wide + ni].astype(F32)
@@ -106,8 +108,8 @@
         for d in far_first(n3):
             y_copy(tbuf.at[d, g, at], r1.at[d - 1, g, at], g * PIECES + lo // ppp, d).start()
 
-    def send_group(g):
-        for p in range(PIECES):
+    def send_group(g, part=0, parts=1):
+        for p in range(part * PIECES // parts, (part + 1) * PIECES // parts):
             send_pairs(g, p * ppp, ppp)
 
     sd = ns // n3
@@ -160,9 +162,6 @@
         sel = onehot(iota((LANES, n3 * nl), 1) == lax.rem(me3 - d + n3, n3) * nl + lax.rem(r, nl))
         w1[d * LANES : (d + 1) * LANES, :] = jnp.where(same_b, dot(sel, cols3), 0.0).astype(BF16)
 
-    for g in range(1, AHEAD):
-        send_group(g)
-
     def stage1(g, p):
         at = pl.ds(p * ppp, ppp)
         y_copy(tbuf.at[pl.ds(1, n3 - 1), g, at], r1.at[:, g, at], g * PIECES + p).wait_recv()
@@ -172,7 +171,7 @@
         width = LANES // bt
         slot = iota((prow, LANES), 1) // width
         at = pl.ds(p * prow, prow)
-        for d in (*far_first(n2), 0):
+        for d in range(n2):
             by_b = [prod[t * prow : (t + 1) * prow, d * LANES : (d + 1) * LANES] for t in range(bt)]
             for u in range(kt):
                 tile = by_b[u]
@@ -180,48 +179,71 @@
                     if t != u:
                         tile = jnp.where(slot == t, pltpu.roll(by_b[t], (t - u) * width % LANES, 1), tile)
                 u3[d, g, at, u * LANES : (u + 1) * LANES] = tile.astype(BF16)
-            if d:
-                x_copy(u3.at[d, g, at], r2.at[d - 1, g, at], g, d).start()
-
-    def stage2(g, final=False):
-        x_copy(u3.at[pl.ds(1, n2 - 1), g], r2.at[:, g], g).wait_recv()
+        for d in far_first(n2):
+            x_copy(u3.at[d, g, at], r2.at[d - 1, g, at], g, d).start()
+
+    def second(g, u, es):
         got = [u3.at[0, g]] + [r2.at[d, g] for d in range(n2 - 1)]
-        for es in ((1,), (0,)) if final else (tuple(range(n1)),):
-            for u in range(kt):
-                rhs = jnp.concatenate([v[:, u * LANES : (u + 1) * LANES] for v in got], axis=1)
-                prod = dot(w2[es[0] * half : (es[-1] + 1) * half, :], rhs, ((1,), (1,))).astype(BF16)
-                at = pl.ds(u * half, half)
-                for k, e in enumerate(es):
-                    if final and e == 0:
-                        last[at, :rows] = prod
-                    else:
-                        v2[e, g, at] = prod[k * half : (k + 1) * half, :]
-                if 1 in es:
-                    c_copy(v2.at[1, g, at], r3.at[g, at], g).start()
-
-    def stage3(g):
-        c_copy(v2.at[1, g], r3.at[g], g).wait_recv()
-        third(jnp.concatenate([v2[0, g], r3[g]], axis=1), w3, dbuf, out, g * SG, (kb, jb, ni))
+        rhs = jnp.concatenate([v[:, u * LANES : (u + 1) * LANES] for v in got], axis=1)
+        prod = dot(w2[es[0] * half : (es[-1] + 1) * half, :], rhs, ((1,), (1,))).astype(BF16)
+        at = pl.ds(u * half, half)
+        for k, e in enumerate(es):
+            v2[e, g, at] = prod[k * half : (k + 1) * half, :]
+        if 1 in es:
+            c_copy(v2.at[1, g, at], r3.at[g, at], g).start()
+
+    def stage2(g, u):
+        if u == 0:
+            x_copy(u3.at[pl.ds(1, n2 - 1), g], r2.at[:, g], g).wait_recv()
+        second(g, u, tuple(range(n1)))
+
+    def stage3(g, part=0, parts=1):
+        if part == 0:
+            c_copy(v2.at[1, g], r3.at[g], g).wait_recv()
+        third(jnp.concatenate([v2[0, g], r3[g]], axis=1), w3, dbuf, out, g * SG, (kb, jb, ni), range(part * SG // 2 // parts, (part + 1) * SG // 2 // parts))
 
     def step(g, carry):
+        def later(p, lag, act):
+            pl.when(g >= lag)(lambda: act(g - lag))
+
         for p in range(PIECES):
             stage1(g, p)
-            if p == PIECES - 2:
-                pl.when(g >= 2)(lambda: stage3(g - 2))
-        pl.when(g + AHEAD < groups)(lambda: send_group(g + AHEAD))
+            if p == 0:
+                later(p, 2, lambda k: stage2(k, 1))
+            if p == FIRST_SEND_AT:
+                for k in range(1, AHEAD):
+                    pl.when(g == 0)(functools.partial(send_group, k))
+            if p in SEND_AT:
+                pl.when(g + AHEAD < groups)(lambda: send_group(g + AHEAD, SEND_AT.index(p), len(SEND_AT)))
+            if p in THIRD_AT:
+                later(p, 3, lambda k: stage3(k, THIRD_AT.index(p), len(THIRD_AT)))
         pl.when(g == 0)(build_rest)
-        pl.when(g >= 1)(lambda: stage2(g - 1))
+        later(p, 1, lambda k: stage2(k, 0))
         return carry
 
     lax.fori_loop(0, groups, step, 0)
-    stage3(groups - 2)
-    stage2(groups - 1, True)
-    c_copy(v2.at[1, groups - 1], r3.at[groups - 1], groups - 1).wait_recv()
-    last[:, rows:] = r3[groups - 1]
+    fin = groups - 1
+    stage2(fin - 1, 1)
+    stage3(fin - 2)
+    stage3(fin - 1)
+    x_copy(u3.at[pl.ds(1, n2 - 1), fin], r2.at[:, fin], fin).wait_recv()
+    for es in ((1,), (0,)):
+        for u in range(kt):
+            second(fin, u, es)
+    last[:, :rows] = v2[0, fin]
+    c_copy(v2.at[1, fin], r3.at[fin], fin).wait_recv()
+    last[:, rows:] = r3[fin]
 
     y_copy(tbuf.at[pl.ds(1, n3 - 1)], r1, 0).wait_send()
     x_copy(u3.at[pl.ds(1, n2 - 1)], r2, 0).wait_send()
     c_copy(v2.at[1], r3, 0).wait_send()
+
+
+def scoped(dims, *refs):
+    dma = pltpu.SemaphoreType.DMA
+    n3, ns = dims[0], dims[6]
+    groups = ns // n3 // SG
+    pl.run_scoped(functools.partial(kernel, dims, *refs), dma((len(FIRST),)), dma((4,)), dma, dma((groups * PIECES,)), dma, dma((groups,)), dma, dma((groups,)))
 
 
 def solution(mesh):
@@ -250,11 +272,10 @@
             pltpu.VMEM(fac_one.shape, BF16),
             pltpu.VMEM(fac_two.shape, BF16),
             pltpu.VMEM(fac_three.shape, BF16),
-            dma((len(FIRST),)), dma((4,)), dma, dma((groups * PIECES,)), dma, dma((groups,)), dma, dma((groups,)),
         ]
         vmem = pl.BlockSpec(memory_space=pltpu.VMEM)
         held = pl.pallas_call(
-            functools.partial(kernel, dims),
+            functools.partial(scoped, dims),
             out_shape=(
                 pltpu.VMEM((ns // n3 - SG, kb, jb, ni), BF16),
                 pltpu.VMEM((kj, n1 * rows), BF16),

time: 65.1 us -> 63.9 us (0.982)
  Pallas kernels: 65 us -> 63.9 us
    pallas_call x1, Pallas kernels: 61.6 us -> 60.5 us  [local_step(): pl.pallas_call(functools.partial(scoped, dims), out_shape=(pltpu.VMEM((ns...]
where the time goes in v4:
time: 63.9 us
  Pallas kernels  63.9 us (100%)
    pallas_call x1, Pallas kernels, local_step(): pl.pallas_call(functools.partial(scoped, dims), out_shape=(pltpu.VMEM((ns...  60.5 us
    pallas_call x1, Pallas kernels, local_step(): pl.pallas_call(finish, out_shape=jax.ShapeDtypeStruct((ns // n3, kb, jb,...  3.37 us

profile of v4, /device:TPU:97, one launch (start us, length us, event | category | flops | bytes accessed | tf_op | source)
XLA Modules:
  0.0 63.9 jit_solution(15505830743583761234)
XLA Ops:
  0.0 60.5 %shard_map.55 = (bf16[56,16,32,64]{3,2,1,0:T(8,128)(2,1)S(1)}, bf16[512,512]{1,0:T(8,128)(2,1)S(1)}, bf16[512,1024]{1,0:T(8,128)(2,1)S(1)}, f32[16,32,64]{2,1,0:T(8,128)S(1)}) custom-call(bf16[32,16,16,256]{3,2,1,0:T(8,128)(2,1)} %bitcast.1, bf16[64,64]{1,0:T(8,128)(2,1)} %refs_1_.1, bf16[64,64]{1,0:T(8,128)(2,1)} %refs_2_.1, bf16[64,64]{1,0:T(8,128)(2,1)} %refs_3_.1, ...), custom_call_target="tpu_custom_call" | custom-call | tf_op jit(solution)/shard_map/pallas_call | solution.py:277
  60.5 3.4 %shard_map.56 = bf16[64,16,32,64]{3,2,1,0:T(8,128)(2,1)} custom-call(bf16[56,16,32,64]{3,2,1,0:T(8,128)(2,1)S(1)} %get-tuple-element.9.done, bf16[512,512]{1,0:T(8,128)(2,1)S(1)} %get-tuple-element.10.last, bf16[512,1024]{1,0:T(8,128)(2,1)S(1)} %get-tuple-element.11.w3, f32[16,32,64]{2,1,0:T(8,128)S(1)} %get-tuple-element.12.d_ref), custom_call_target="tpu_custom_call" | custom-call | tf_op jit(solution)/shard_map/pallas_call | solution.py:290

commit v5 on v4

--- a/solution.py
+++ b/solution.py
@@ -10,11 +10,14 @@
 MESH = pl.DeviceIdType.MESH
 BF16, F32 = jnp.bfloat16, jnp.float32
 SG = 8
-PIECES = 8
-FIRST = (1, 1) + (2,) * 7
-COPIES = 7
-FIRST_SEND_AT = 0
-SEND_AT, THIRD_AT = (2,), (3,)
+SIZES = (2,) * 8
+PIECES = len(SIZES)
+STARTS = tuple(sum(SIZES[:i]) for i in range(PIECES))
+FIRST = (1, 1, 2, 4, 4, 4)
+COPIES = 6
+LATE = 2
+FIRST_SEND_AT = 2
+SEND_AT, THIRD_AT = (5,), (3,)
 AHEAD = 2
 LANES = 128
 
@@ -52,9 +55,10 @@
     copies = [pltpu.make_async_copy(done.at[pl.ds(i * chunk, chunk)], out.at[pl.ds(i * chunk, chunk)], sem.at[i]) for i in range(COPIES)]
     for c in copies:
         c.start()
-    third(last[...], w3, d_ref, tail, 0, tail.shape[1:])
-    copies.append(pltpu.make_async_copy(tail, out.at[pl.ds(size, SG)], sem.at[COPIES]))
-    copies[-1].start()
+    for k in range(LATE):
+        third(last[k], w3, d_ref, tail, k * SG, tail.shape[1:])
+        copies.append(pltpu.make_async_copy(tail.at[pl.ds(k * SG, SG)], out.at[pl.ds(size + k * SG, SG)], sem.at[COPIES + k]))
+        copies[-1].start()
     for c in copies:
         c.wait()
 
@@ -66,8 +70,6 @@
     groups = ns // n3 // SG
     rows = na * SG
     pairs = na // 2
-    ppp = pairs // PIECES
-    prow = rows // PIECES
     kb, jb = nk // n2, nj // n1
     bl, bk, kj = nb * nl, nb * kb, kb * jb
     bt, kt = bl // LANES, bk // LANES
@@ -84,9 +86,10 @@
 
     barrier = pltpu.get_barrier_semaphore()
     peers = 0
-    for axis, me, n in (("m3", me3, n3), ("m2", me2, n2), ("m1", me1, n1)):
-        for d in range(1, n):
-            pl.semaphore_signal(barrier, inc=1, device_id={axis: lax.rem(me + d, n)}, device_id_type=MESH)
+    other = lax.rem(me1 + 1, n1)
+    for axis, me, n, core, first in (("m3", me3, n3, me1, 1), ("m2", me2, n2, other, 0)):
+        for d in range(first, n):
+            pl.semaphore_signal(barrier, inc=1, device_id={axis: lax.rem(me + d, n), "m1": core}, device_id_type=MESH)
             peers += 1
     for f in loads[1:] + facs:
         f.start()
@@ -97,20 +100,20 @@
 
     def x_copy(src, dst, sem, d=1):
         return pltpu.make_async_remote_copy(src_ref=src, dst_ref=dst, send_sem=x_send, recv_sem=x_recv.at[sem],
-                                            device_id={"m2": lax.rem(me2 + d, n2)}, device_id_type=MESH)
+                                            device_id={"m2": lax.rem(me2 + d, n2), "m1": other}, device_id_type=MESH)
 
     def c_copy(src, dst, sem):
         return pltpu.make_async_remote_copy(src_ref=src, dst_ref=dst, send_sem=c_send, recv_sem=c_recv.at[sem],
-                                            device_id={"m1": lax.rem(me1 + 1, n1)}, device_id_type=MESH)
-
-    def send_pairs(g, lo, n):
+                                            device_id={"m1": other}, device_id_type=MESH)
+
+    def send_pairs(g, lo, n, p):
         at = pl.ds(lo, n)
         for d in far_first(n3):
-            y_copy(tbuf.at[d, g, at], r1.at[d - 1, g, at], g * PIECES + lo // ppp, d).start()
+            y_copy(tbuf.at[d, g, at], r1.at[d - 1, g, at], g * PIECES + p, d).start()
 
     def send_group(g, part=0, parts=1):
         for p in range(part * PIECES // parts, (part + 1) * PIECES // parts):
-            send_pairs(g, p * ppp, ppp)
+            send_pairs(g, STARTS[p], SIZES[p], p)
 
     sd = ns // n3
     r, c = iota((ns, ns), 0), iota((ns, ns), 1)
@@ -136,7 +139,7 @@
         same_s = lax.rem(r, SG) == c // wide
         for e in range(n1):
             r = iota((rows, n1 * na), 0)
-            sel = onehot(iota((rows, n1 * na), 1) == lax.rem(me1 + e, n1) * na + r // SG)
+            sel = onehot(iota((rows, n1 * na), 1) == lax.rem(me1 + 1 + e, n1) * na + r // SG)
             w3[e * rows : (e + 1) * rows, :] = jnp.where(same_s, dot(sel, cols1), 0.0).astype(BF16)
 
     wide = 2 * ni
@@ -148,7 +151,10 @@
             tbuf[:, :, ap] = jnp.stack(two, axis=1).reshape(n3, groups, 2 * SG, bl).astype(BF16)
         if h == 0:
             pl.semaphore_wait(barrier, peers)
-        send_pairs(0, cuts[h], n)
+        for p in range(PIECES):
+            lo, hi = max(cuts[h], STARTS[p]), min(cuts[h + 1], STARTS[p] + SIZES[p])
+            if lo < hi:
+                send_pairs(0, lo, hi - lo, p)
 
     c = iota((nk, n2 * LANES), 1)
     k_of = lax.rem(c, LANES) // (LANES // kt) * ks + lax.rem(c, ks)
@@ -163,14 +169,14 @@
         w1[d * LANES : (d + 1) * LANES, :] = jnp.where(same_b, dot(sel, cols3), 0.0).astype(BF16)
 
     def stage1(g, p):
-        at = pl.ds(p * ppp, ppp)
+        at, prow = pl.ds(STARTS[p], SIZES[p]), 2 * SG * SIZES[p]
         y_copy(tbuf.at[pl.ds(1, n3 - 1), g, at], r1.at[:, g, at], g * PIECES + p).wait_recv()
         got = [tbuf[0, g, at].reshape(prow, bl)] + [r1[d, g, at].reshape(prow, bl) for d in range(n3 - 1)]
         lhs = [jnp.concatenate([v[:, t * LANES : (t + 1) * LANES] for v in got], axis=1) for t in range(bt)]
         prod = dot(jnp.concatenate(lhs, axis=0), w1[...])
         width = LANES // bt
         slot = iota((prow, LANES), 1) // width
-        at = pl.ds(p * prow, prow)
+        at = pl.ds(STARTS[p] * 2 * SG, prow)
         for d in range(n2):
             by_b = [prod[t * prow : (t + 1) * prow, d * LANES : (d + 1) * LANES] for t in range(bt)]
             for u in range(kt):
@@ -179,22 +185,27 @@
                     if t != u:
                         tile = jnp.where(slot == t, pltpu.roll(by_b[t], (t - u) * width % LANES, 1), tile)
                 u3[d, g, at, u * LANES : (u + 1) * LANES] = tile.astype(BF16)
-        for d in far_first(n2):
-            x_copy(u3.at[d, g, at], r2.at[d - 1, g, at], g, d).start()
-
-    def second(g, u, es):
-        got = [u3.at[0, g]] + [r2.at[d, g] for d in range(n2 - 1)]
+        for d in (*far_first(n2), 0):
+            x_copy(u3.at[d, g, at], r2.at[d, g, at], 2 * g + 2 * p // PIECES, d).start()
+
+    def x_wait(g, part):
+        at = pl.ds(part * rows // 2, rows // 2)
+        x_copy(u3.at[:, g, at], r2.at[:, g, at], 2 * g + part).wait_recv()
+
+    def second(g, u, es, col=slice(None), send=True):
+        got = [r2.at[d, g, col] for d in range(n2)]
         rhs = jnp.concatenate([v[:, u * LANES : (u + 1) * LANES] for v in got], axis=1)
         prod = dot(w2[es[0] * half : (es[-1] + 1) * half, :], rhs, ((1,), (1,))).astype(BF16)
         at = pl.ds(u * half, half)
         for k, e in enumerate(es):
-            v2[e, g, at] = prod[k * half : (k + 1) * half, :]
-        if 1 in es:
-            c_copy(v2.at[1, g, at], r3.at[g, at], g).start()
+            v2[e, g, at, col] = prod[k * half : (k + 1) * half, :]
+        if 1 in es and send:
+            c_copy(v2.at[1, g, at, col], r3.at[g, at, col], g).start()
 
     def stage2(g, u):
         if u == 0:
-            x_copy(u3.at[pl.ds(1, n2 - 1), g], r2.at[:, g], g).wait_recv()
+            for part in range(2):
+                x_wait(g, part)
         second(g, u, tuple(range(n1)))
 
     def stage3(g, part=0, parts=1):
@@ -225,17 +236,25 @@
     fin = groups - 1
     stage2(fin - 1, 1)
     stage3(fin - 2)
-    stage3(fin - 1)
-    x_copy(u3.at[pl.ds(1, n2 - 1), fin], r2.at[:, fin], fin).wait_recv()
-    for es in ((1,), (0,)):
+    def hand_over(g):
+        c_copy(v2.at[1, g], r3.at[g], g).wait_recv()
+        last[g - groups + LATE, :, :rows] = v2[0, g]
+        last[g - groups + LATE, :, rows:] = r3[g]
+
+    for part in range(2):
+        x_wait(fin, part)
+        col = pl.ds(part * rows // 2, rows // 2)
         for u in range(kt):
-            second(fin, u, es)
-    last[:, :rows] = v2[0, fin]
-    c_copy(v2.at[1, fin], r3.at[fin], fin).wait_recv()
-    last[:, rows:] = r3[fin]
+            second(fin, u, (1,), col, False)
+        c_copy(v2.at[1, fin, :, col], r3.at[fin, :, col], fin).start()
+        if part == 0:
+            hand_over(fin - 1)
+    for u in range(kt):
+        second(fin, u, (0,))
+    hand_over(fin)
 
     y_copy(tbuf.at[pl.ds(1, n3 - 1)], r1, 0).wait_send()
-    x_copy(u3.at[pl.ds(1, n2 - 1)], r2, 0).wait_send()
+    x_copy(u3, r2, 0).wait_send()
     c_copy(v2.at[1], r3, 0).wait_send()
 
 
@@ -243,7 +262,7 @@
     dma = pltpu.SemaphoreType.DMA
     n3, ns = dims[0], dims[6]
     groups = ns // n3 // SG
-    pl.run_scoped(functools.partial(kernel, dims, *refs), dma((len(FIRST),)), dma((4,)), dma, dma((groups * PIECES,)), dma, dma((groups,)), dma, dma((groups,)))
+    pl.run_scoped(functools.partial(kernel, dims, *refs), dma((len(FIRST),)), dma((4,)), dma, dma((groups * PIECES,)), dma, dma((2 * groups,)), dma, dma((groups,)))
 
 
 def solution(mesh):
@@ -263,7 +282,7 @@
             pltpu.VMEM((n3, groups, na // 2, 2 * SG, bl), BF16),
             pltpu.VMEM((n3 - 1, groups, na // 2, 2 * SG, bl), BF16),
             pltpu.VMEM((n2, groups, rows, bk), BF16),
-            pltpu.VMEM((n2 - 1, groups, rows, bk), BF16),
+            pltpu.VMEM((n2, groups, rows, bk), BF16),
             pltpu.VMEM((n1, groups, kj, rows), BF16),
             pltpu.VMEM((groups, kj, rows), BF16),
             pltpu.VMEM((n3 * LANES, n2 * LANES), BF16),
@@ -277,8 +296,8 @@
         held = pl.pallas_call(
             functools.partial(scoped, dims),
             out_shape=(
-                pltpu.VMEM((ns // n3 - SG, kb, jb, ni), BF16),
-                pltpu.VMEM((kj, n1 * rows), BF16),
+                pltpu.VMEM((ns // n3 - LATE * SG, kb, jb, ni), BF16),
+                pltpu.VMEM((LATE, kj, n1 * rows), BF16),
                 pltpu.VMEM((n1 * rows, SG * 2 * ni), BF16),
                 pltpu.VMEM(diag_blk.shape, F32),
             ),
@@ -292,7 +311,7 @@
             out_shape=jax.ShapeDtypeStruct((ns // n3, kb, jb, ni), BF16),
             in_specs=[vmem] * 4,
             out_specs=any_space,
-            scratch_shapes=[pltpu.VMEM((SG, kb, jb, ni), BF16), dma((COPIES + 1,))],
+            scratch_shapes=[pltpu.VMEM((LATE * SG, kb, jb, ni), BF16), dma((COPIES + LATE,))],
             compiler_params=pltpu.CompilerParams(vmem_limit_bytes=12 * 1024 * 1024),
         )(*held)
 

time: 63.9 us -> 63.2 us (0.989)
  Pallas kernels: 63.9 us -> 63.1 us
    pallas_call x1, Pallas kernels: 60.5 us -> 59.8 us  [local_step(): pl.pallas_call(functools.partial(scoped, dims), out_shape=(pltpu.VMEM((ns...]
where the time goes in v5:
time: 63.2 us; the launch traced here: 63.1 us
  Pallas kernels  63.1 us (100%)
    pallas_call x1, Pallas kernels, local_step(): pl.pallas_call(functools.partial(scoped, dims), out_shape=(pltpu.VMEM((ns...  59.8 us
    pallas_call x1, Pallas kernels, local_step(): pl.pallas_call(finish, out_shape=jax.ShapeDtypeStruct((ns // n3, kb, jb,...  3.37 us

profile of v5, /device:TPU:97, one launch (start us, length us, event | category | flops | bytes accessed | tf_op | source)
XLA Modules:
  0.0 63.1 jit_solution(16729222124528714249)
XLA Ops:
  0.0 59.8 %shard_map.55 = (bf16[48,16,32,64]{3,2,1,0:T(8,128)(2,1)S(1)}, bf16[2,512,512]{2,1,0:T(8,128)(2,1)S(1)}, bf16[512,1024]{1,0:T(8,128)(2,1)S(1)}, f32[16,32,64]{2,1,0:T(8,128)S(1)}) custom-call(bf16[32,16,16,256]{3,2,1,0:T(8,128)(2,1)} %bitcast.1, bf16[64,64]{1,0:T(8,128)(2,1)} %refs_1_.1, bf16[64,64]{1,0:T(8,128)(2,1)} %refs_2_.1, bf16[64,64]{1,0:T(8,128)(2,1)} %refs_3_.1, ...), custom_call_target="tpu_custom_call" | custom-call | tf_op jit(solution)/shard_map/pallas_call | solution.py:296
  59.8 3.4 %shard_map.56 = bf16[64,16,32,64]{3,2,1,0:T(8,128)(2,1)} custom-call(bf16[48,16,32,64]{3,2,1,0:T(8,128)(2,1)S(1)} %get-tuple-element.9.done, bf16[2,512,512]{2,1,0:T(8,128)(2,1)S(1)} %get-tuple-element.10.last, bf16[512,1024]{1,0:T(8,128)(2,1)S(1)} %get-tuple-element.11.w3, f32[16,32,64]{2,1,0:T(8,128)S(1)} %get-tuple-element.12.d_ref), custom_call_target="tpu_custom_call" | custom-call | tf_op jit(solution)/shard_map/pallas_call | solution.py:309

commit v6 on v5

--- a/solution.py
+++ b/solution.py
@@ -14,10 +14,10 @@
 PIECES = len(SIZES)
 STARTS = tuple(sum(SIZES[:i]) for i in range(PIECES))
 FIRST = (1, 1, 2, 4, 4, 4)
-COPIES = 6
+COPIES = 3
 LATE = 2
 FIRST_SEND_AT = 2
-SEND_AT, THIRD_AT = (5,), (3,)
+SEND_AT, THIRD_AT = (5, 6), (2, 3)
 AHEAD = 2
 LANES = 128
 
@@ -186,7 +186,7 @@
                         tile = jnp.where(slot == t, pltpu.roll(by_b[t], (t - u) * width % LANES, 1), tile)
                 u3[d, g, at, u * LANES : (u + 1) * LANES] = tile.astype(BF16)
         for d in (*far_first(n2), 0):
-            x_copy(u3.at[d, g, at], r2.at[d, g, at], 2 * g + 2 * p // PIECES, d).start()
+            x_copy(u3.at[d, g, at], r2.at[d, g, at], 2 * g + 2 * STARTS[p] // pairs, d).start()
 
     def x_wait(g, part):
         at = pl.ds(part * rows // 2, rows // 2)

time: 63.2 us -> 63.2 us (level)
  no operation moved by 1% of the time
where the time goes in v6:
time: 63.2 us; the launch traced here: 63.1 us
  Pallas kernels  63.1 us (100%)
    pallas_call x1, Pallas kernels, local_step(): pl.pallas_call(functools.partial(scoped, dims), out_shape=(pltpu.VMEM((ns...  59.8 us
    pallas_call x1, Pallas kernels, local_step(): pl.pallas_call(finish, out_shape=jax.ShapeDtypeStruct((ns // n3, kb, jb,...  3.34 us

profile of v6, /device:TPU:97, one launch (start us, length us, event | category | flops | bytes accessed | tf_op | source)
XLA Modules:
  0.0 63.1 jit_solution(6544249645702634885)
XLA Ops:
  0.0 59.8 %shard_map.55 = (bf16[48,16,32,64]{3,2,1,0:T(8,128)(2,1)S(1)}, bf16[2,512,512]{2,1,0:T(8,128)(2,1)S(1)}, bf16[512,1024]{1,0:T(8,128)(2,1)S(1)}, f32[16,32,64]{2,1,0:T(8,128)S(1)}) custom-call(bf16[32,16,16,256]{3,2,1,0:T(8,128)(2,1)} %bitcast.1, bf16[64,64]{1,0:T(8,128)(2,1)} %refs_1_.1, bf16[64,64]{1,0:T(8,128)(2,1)} %refs_2_.1, bf16[64,64]{1,0:T(8,128)(2,1)} %refs_3_.1, ...), custom_call_target="tpu_custom_call" | custom-call | tf_op jit(solution)/shard_map/pallas_call | solution.py:296
  59.8 3.3 %shard_map.56 = bf16[64,16,32,64]{3,2,1,0:T(8,128)(2,1)} custom-call(bf16[48,16,32,64]{3,2,1,0:T(8,128)(2,1)S(1)} %get-tuple-element.9.done, bf16[2,512,512]{2,1,0:T(8,128)(2,1)S(1)} %get-tuple-element.10.last, bf16[512,1024]{1,0:T(8,128)(2,1)S(1)} %get-tuple-element.11.w3, f32[16,32,64]{2,1,0:T(8,128)S(1)} %get-tuple-element.12.d_ref), custom_call_target="tpu_custom_call" | custom-call | tf_op jit(solution)/shard_map/pallas_call | solution.py:309

commit v7 on v6

--- a/solution.py
+++ b/solution.py
@@ -82,12 +82,12 @@
         loads.append(pltpu.make_async_copy(x_hbm.at[part], xbuf.at[part], in_sem.at[len(loads)]))
         cuts.append(cuts[-1] + n)
     facs = [pltpu.make_async_copy(s, t, fac_sem.at[i]) for i, (s, t) in enumerate(((a3_hbm, a3), (a2_hbm, a2), (a1_hbm, a1), (d_hbm, dbuf)))]
-    loads[0].start()
-
     barrier = pltpu.get_barrier_semaphore()
     peers = 0
     other = lax.rem(me1 + 1, n1)
     for axis, me, n, core, first in (("m3", me3, n3, me1, 1), ("m2", me2, n2, other, 0)):
+        if axis == "m2":
+            loads[0].start()
         for d in range(first, n):
             pl.semaphore_signal(barrier, inc=1, device_id={axis: lax.rem(me + d, n), "m1": core}, device_id_type=MESH)
             peers += 1

time: 63.2 us -> 63.2 us (level)
  no operation moved by 1% of the time
where the time goes in v7:
time: 63.2 us; the launch traced here: 63.1 us
  Pallas kernels  63.1 us (100%)
    pallas_call x1, Pallas kernels, local_step(): pl.pallas_call(functools.partial(scoped, dims), out_shape=(pltpu.VMEM((ns...  59.7 us
    pallas_call x1, Pallas kernels, local_step(): pl.pallas_call(finish, out_shape=jax.ShapeDtypeStruct((ns // n3, kb, jb,...  3.34 us

profile of v7, /device:TPU:97, one launch (start us, length us, event | category | flops | bytes accessed | tf_op | source)
XLA Modules:
  0.0 63.1 jit_solution(1239034422971610171)
XLA Ops:
  0.0 59.7 %shard_map.55 = (bf16[48,16,32,64]{3,2,1,0:T(8,128)(2,1)S(1)}, bf16[2,512,512]{2,1,0:T(8,128)(2,1)S(1)}, bf16[512,1024]{1,0:T(8,128)(2,1)S(1)}, f32[16,32,64]{2,1,0:T(8,128)S(1)}) custom-call(bf16[32,16,16,256]{3,2,1,0:T(8,128)(2,1)} %bitcast.1, bf16[64,64]{1,0:T(8,128)(2,1)} %refs_1_.1, bf16[64,64]{1,0:T(8,128)(2,1)} %refs_2_.1, bf16[64,64]{1,0:T(8,128)(2,1)} %refs_3_.1, ...), custom_call_target="tpu_custom_call" | custom-call | tf_op jit(solution)/shard_map/pallas_call | solution.py:296
  59.7 3.3 %shard_map.56 = bf16[64,16,32,64]{3,2,1,0:T(8,128)(2,1)} custom-call(bf16[48,16,32,64]{3,2,1,0:T(8,128)(2,1)S(1)} %get-tuple-element.9.done, bf16[2,512,512]{2,1,0:T(8,128)(2,1)S(1)} %get-tuple-element.10.last, bf16[512,1024]{1,0:T(8,128)(2,1)S(1)} %get-tuple-element.11.w3, f32[16,32,64]{2,1,0:T(8,128)S(1)} %get-tuple-element.12.d_ref), custom_call_target="tpu_custom_call" | custom-call | tf_op jit(solution)/shard_map/pallas_call | solution.py:309

commit v8 on v7

--- a/solution.py
+++ b/solution.py
@@ -13,7 +13,7 @@
 SIZES = (2,) * 8
 PIECES = len(SIZES)
 STARTS = tuple(sum(SIZES[:i]) for i in range(PIECES))
-FIRST = (1, 1, 2, 4, 4, 4)
+FIRST = (1, 1, 1, 1, 4, 8)
 COPIES = 3
 LATE = 2
 FIRST_SEND_AT = 2

time: 63.2 us -> 63.1 us (level)
  no operation moved by 1% of the time
where the time goes in v8:
time: 63.1 us
  Pallas kernels  63.1 us (100%)
    pallas_call x1, Pallas kernels, local_step(): pl.pallas_call(functools.partial(scoped, dims), out_shape=(pltpu.VMEM((ns...  59.7 us
    pallas_call x1, Pallas kernels, local_step(): pl.pallas_call(finish, out_shape=jax.ShapeDtypeStruct((ns // n3, kb, jb,...  3.34 us

profile of v8, /device:TPU:97, one launch (start us, length us, event | category | flops | bytes accessed | tf_op | source)
XLA Modules:
  0.0 63.1 jit_solution(1066010711665244427)
XLA Ops:
  0.0 59.7 %shard_map.55 = (bf16[48,16,32,64]{3,2,1,0:T(8,128)(2,1)S(1)}, bf16[2,512,512]{2,1,0:T(8,128)(2,1)S(1)}, bf16[512,1024]{1,0:T(8,128)(2,1)S(1)}, f32[16,32,64]{2,1,0:T(8,128)S(1)}) custom-call(bf16[32,16,16,256]{3,2,1,0:T(8,128)(2,1)} %bitcast.1, bf16[64,64]{1,0:T(8,128)(2,1)} %refs_1_.1, bf16[64,64]{1,0:T(8,128)(2,1)} %refs_2_.1, bf16[64,64]{1,0:T(8,128)(2,1)} %refs_3_.1, ...), custom_call_target="tpu_custom_call" | custom-call | tf_op jit(solution)/shard_map/pallas_call | solution.py:296
  59.7 3.3 %shard_map.56 = bf16[64,16,32,64]{3,2,1,0:T(8,128)(2,1)} custom-call(bf16[48,16,32,64]{3,2,1,0:T(8,128)(2,1)S(1)} %get-tuple-element.9.done, bf16[2,512,512]{2,1,0:T(8,128)(2,1)S(1)} %get-tuple-element.10.last, bf16[512,1024]{1,0:T(8,128)(2,1)S(1)} %get-tuple-element.11.w3, f32[16,32,64]{2,1,0:T(8,128)S(1)} %get-tuple-element.12.d_ref), custom_call_target="tpu_custom_call" | custom-call | tf_op jit(solution)/shard_map/pallas_call | solution.py:309
